TPU v7x, 512 devices: a 8x2x16 block of a 8x8x16 slice. The times are simulated.
512 devices in a mesh: rep: 2 (over y), seq: 16 (over z), head: 8 (over x), sub: 2 (over core).
Axes of the slice: x: 8, y: 2, z: 16, core: 2. Of those that a mesh axis runs over, the one named last changes fastest.
The devices are a block of a 8x8x16 slice.
Arguments:
- tokens: bfloat16 [32, 4096], P(('rep', 'sub'), 'seq'), parts along dimension 0, may hold values from -260 to 260
- attn_gain: float32 [4096], P('seq'), may hold values from 0.1 to 1.9
- w_query: bfloat16 [4096, 4096], P('seq', 'head'), may hold values from -0.09375 to 0.09375
- key_projection_weight: bfloat16 [4096, 1024], P('seq', 'head'), may hold values from -0.375 to 0.375
- value_projection_weight: bfloat16 [4096, 1024], P('seq', 'head'), may hold values from -0.375 to 0.375
- w_attn_out: bfloat16 [4096, 4096], P('head', 'seq'), may hold values from -0.09375 to 0.09375
- cache_keys: bfloat16 [32, 8, 8192, 128], P(('rep', 'sub'), 'head', 'seq'), parts along dimension 0, may hold values from -2500 to 2500
- stored_value_cache: bfloat16 [32, 8, 8192, 128], P(('rep', 'sub'), 'head', 'seq'), parts along dimension 0, may hold values from -12 to 12
- lengths: int32 [32], P(('rep', 'sub')), parts along dimension 0, may hold values from 4096 to 8192
- positions: int32 [32], P(('rep', 'sub')), parts along dimension 0, may hold values from 0 to 8191
- mamba_gain: float32 [4096], replicated, may hold values from 0.1 to 1.9
- w_in: bfloat16 [2, 4096, 8192], P(None, None, ('seq', 'head')), may hold values from -0.09375 to 0.09375
- conv_weight: float32 [4, 8192], P(None, ('seq', 'head')), may hold values from -3 to 3
- conv_bias: float32 [8192], P(('seq', 'head')), may hold values from -0.5 to 0.5
- conv_state: float32 [32, 3, 8192], P(('rep', 'sub'), None, ('seq', 'head')), parts along dimension 0, may hold values from -6 to 6
- w_xproj: bfloat16 [8192, 288], P(('seq', 'head')), may hold values from -0.0625 to 0.0625
- w_dt: bfloat16 [256, 8192], P(None, ('seq', 'head')), may hold values from -0.375 to 0.375
- dt_bias: float32 [8192], P(('seq', 'head')), may hold values from -4 to 0
- a_log: float32 [16, 8192], P(None, ('seq', 'head')), may hold values from 0 to 2.77
- skip_gain: float32 [8192], P(('seq', 'head')), may hold values from 0.25 to 2
- ssm_state: float32 [32, 16, 8192], P(('rep', 'sub'), None, ('seq', 'head')), parts along dimension 0, may hold values from -6 to 6
- w_mamba_out: bfloat16 [8192, 4096], P(('seq', 'head')), may hold values from -0.25 to 0.25
Outputs:
- hidden_out: bfloat16 [32, 4096], P(('rep', 'sub'), 'seq'), parts along dimension 0
- new_state: float32 [32, 16, 8192], P(('rep', 'sub'), None, ('seq', 'head')), parts along dimension 0
There are 2 independent parts, one for each index of `rep`. A program takes and returns all parts, laid end to end along the dimension named above; an argument that names none is the same for every part. Nothing has to cross between parts.
Inputs may be any that keep to these rules, and one draw needn't show every extreme that they name: Cache positions p < lengths[b] hold sequence b's past keys and values; later positions are not attended.
All inputs are finite; a program needn't handle non-finite values.
Results may differ from a plain program's by a relative error of at most 0.015.
Values may be sent and summed in bfloat16 or wider, within the bound.
A program may use at most 64 MiB of HBM per device.

v0:
```python
import math

import jax
import jax.numpy as jnp
from jax import lax
from jax.sharding import PartitionSpec as P

norm_eps = 1e-05
masked_floor = -1e30
rope_base = 10000.0


def copy_for_each(value, axis):
    peers = lax.axis_size(axis)
    return lax.all_to_all(
        jnp.broadcast_to(value[None], (peers, *value.shape)), axis, 0, 0, tiled=True
    )


def taken_together(value, axis):
    everything = copy_for_each(value, axis)
    return jnp.sum(everything, axis=0)


def together(arrays, axis):
    line, at, done = (jnp.concatenate([a.reshape(-1) for a in arrays]), 0, [])
    subtotal = taken_together(line, axis)
    for a in arrays:
        done.append(subtotal[at : at + a.size].reshape(a.shape))
        at += a.size
    return tuple(done)


def gathered_once(value, axis):
    leaves = jax.tree.leaves(value)
    turns = sorted(range(len(leaves)), key=lambda k: -leaves[k].size)
    width = (1, *leaves[turns[0]].shape)[-1]
    lines = [
        jnp.pad(leaves[k].reshape(-1), (0, -leaves[k].size % width)).reshape(-1, width)
        for k in turns
    ]
    both, at, found = (copy_for_each(jnp.concatenate(lines), axis), 0, {})
    for k, line in zip(turns, lines):
        section = both[:, at : at + len(line)].reshape(len(both), -1)
        found[k] = section[:, : leaves[k].size].reshape(-1, *leaves[k].shape)
        at += len(line)
    numbers = iter(range(len(leaves)))
    return jax.tree.map(lambda _: found[next(numbers)], value)


def combined_pairwise(pieces, combine):
    while len(jax.tree.leaves(pieces)[0]) > 1:
        pieces = jax.vmap(combine)(
            *(jax.tree.map(lambda part: part[side::2], pieces) for side in (0, 1))
        )
    return jax.tree.map(lambda part: part[0], pieces)


def merged(value, axis, combine):
    pieces = gathered_once(value, axis)
    return combined_pairwise(pieces, combine)


def in_order(blocks, dim):
    blocks = jnp.moveaxis(blocks, 0, dim)
    dims = blocks.shape
    return blocks.reshape(*dims[:dim], dims[dim] * dims[dim + 1], *dims[dim + 2 :])


def collect(value, axis, dim):
    return in_order(copy_for_each(value, axis), dim)


def over_axes(value, axes):
    for axis in axes:
        value = lax.psum(value, axis)
    return value


def in_blocks(value, dim, peers):
    dims = value.shape
    blocks = value.reshape(*dims[:dim], peers, dims[dim] // peers, *dims[dim + 1 :])
    return jnp.moveaxis(blocks, dim, 0)


def sent_and_summed(value, axis, dim):
    peers = lax.axis_size(axis)
    blocks = lax.all_to_all(in_blocks(value, dim, peers), axis, 0, 0, tiled=True)
    return jnp.sum(blocks.astype(jnp.float32), axis=0)


def apply_rotary(vectors, positions):
    half_dim = vectors.shape[-1] // 2
    frequency = jnp.exp(
        -math.log(rope_base) * 2.0 * jnp.arange(half_dim, dtype=jnp.float32) / (2 * half_dim)
    )
    angles = positions.astype(jnp.float32)[:, None] * frequency[None, :]
    cosine = jnp.cos(angles)[:, None, :]
    sine_part = jnp.sin(angles)[:, None, :]
    first_half = vectors[..., :half_dim]
    second_half = vectors[..., half_dim:]
    return jnp.concatenate(
        [
            first_half * cosine - second_half * sine_part,
            second_half * cosine + first_half * sine_part,
        ],
        axis=-1,
    )


def join_partial(earlier, later):
    max_one, sum_one, acc_one = earlier
    max_two, sum_two, acc_two = later
    joined_max = jnp.maximum(max_one, max_two)
    factor_one = jnp.exp(max_one - joined_max)
    factor_two = jnp.exp(max_two - joined_max)
    return (
        joined_max,
        sum_one * factor_one + sum_two * factor_two,
        acc_one * factor_one[..., None] + acc_two * factor_two[..., None],
    )


def local(
    tokens,
    attn_gain,
    w_query,
    key_projection_weight,
    value_projection_weight,
    w_attn_out,
    cache_keys,
    stored_value_cache,
    lengths,
    positions,
    mamba_gain,
    w_in,
    conv_weight,
    conv_bias,
    conv_state,
    w_xproj,
    w_dt,
    dt_bias,
    a_log,
    skip_gain,
    ssm_state,
    w_mamba_out,
):
    batch_rows = tokens.shape[0]
    feature_cols = tokens.shape[1]
    head_dim = cache_keys.shape[3]
    kv_local = cache_keys.shape[1]
    ctx_local = cache_keys.shape[2]
    q_local = w_query.shape[1] // head_dim
    query_group_count = q_local // kv_local
    model_width = feature_cols * lax.axis_size("seq")
    token_float = tokens.astype(jnp.float32)
    lifted = (token_float * attn_gain[None, :]).astype(jnp.bfloat16)
    part_query = jnp.dot(lifted, w_query, preferred_element_type=jnp.float32)
    part_key = jnp.dot(lifted, key_projection_weight, preferred_element_type=jnp.float32)
    part_value = jnp.dot(lifted, value_projection_weight, preferred_element_type=jnp.float32)
    squares = jnp.sum(token_float * token_float, axis=1)
    part_query, part_key, part_value, sum_squares = together(
        (part_query, part_key, part_value, squares), "seq"
    )
    inv_rms = lax.rsqrt(sum_squares / model_width + norm_eps)
    query_vectors = apply_rotary(
        (part_query * inv_rms[:, None]).reshape(batch_rows, q_local, head_dim), positions
    ).astype(jnp.bfloat16)
    fresh_key_rows = apply_rotary(
        (part_key * inv_rms[:, None]).reshape(batch_rows, kv_local, head_dim), positions
    ).astype(jnp.bfloat16)
    fresh_value_rows = (
        (part_value * inv_rms[:, None]).reshape(batch_rows, kv_local, head_dim).astype(jnp.bfloat16)
    )
    grouped_queries = query_vectors.reshape(batch_rows, kv_local, query_group_count, head_dim)
    score_scale = head_dim ** (-0.5)
    scores = (
        jnp.einsum(
            "bhgd,bhtd->bhgt", grouped_queries, cache_keys, preferred_element_type=jnp.float32
        )
        * score_scale
    )
    slot_index = lax.axis_index("seq") * ctx_local + jnp.arange(ctx_local, dtype=jnp.int32)
    live_mask = slot_index[None, None, None, :] < lengths[:, None, None, None]
    local_max = jnp.max(jnp.where(live_mask, scores, masked_floor), axis=-1)
    weights = jnp.where(live_mask, jnp.exp(scores - local_max[..., None]), 0.0)
    local_sum = jnp.sum(weights, axis=-1)
    local_acc = jnp.einsum(
        "bhgt,bhtd->bhgd",
        weights.astype(jnp.bfloat16),
        stored_value_cache,
        preferred_element_type=jnp.float32,
    )
    merged_max, merged_sum, merged_acc = merged(
        (local_max, local_sum, local_acc), "seq", join_partial
    )
    score_new = (
        jnp.einsum(
            "bhgd,bhd->bhg", grouped_queries.astype(jnp.float32), fresh_key_rows.astype(jnp.float32)
        )
        * score_scale
    )
    row_max = jnp.maximum(merged_max, score_new)
    old_factor = jnp.exp(merged_max - row_max)
    new_weight = jnp.exp(score_new - row_max)
    total_weight = merged_sum * old_factor + new_weight
    attended = (
        merged_acc * old_factor[..., None]
        + new_weight[..., None] * fresh_value_rows.astype(jnp.float32)[:, :, None, :]
    )
    attn_rows = (
        (attended / total_weight[..., None])
        .reshape(batch_rows, q_local * head_dim)
        .astype(jnp.bfloat16)
    )
    out_part = jnp.dot(attn_rows, w_attn_out, preferred_element_type=jnp.float32)
    summed = taken_together(out_part, "head")
    mid_stream = (token_float + summed).astype(jnp.bfloat16)
    full_tokens = collect(mid_stream, "seq", 1)
    full_float = full_tokens.astype(jnp.float32)
    inv_rms_two = lax.rsqrt(jnp.mean(full_float * full_float, axis=1) + norm_eps)
    lifted_two = (full_float * inv_rms_two[:, None] * mamba_gain[None, :]).astype(jnp.bfloat16)
    inner = jnp.dot(lifted_two, w_in[0], preferred_element_type=jnp.float32)
    gate_branch = jnp.dot(lifted_two, w_in[1], preferred_element_type=jnp.float32)
    window = jnp.concatenate([conv_state, inner[:, None, :]], axis=1)
    mixed = jnp.sum(window * conv_weight[None, :, :], axis=1) + conv_bias[None, :]
    activated = jax.nn.silu(mixed)
    proj_part = jnp.dot(activated.astype(jnp.bfloat16), w_xproj, preferred_element_type=jnp.float32)
    projected = over_axes(proj_part, ("seq", "head"))
    rank_width = w_dt.shape[0]
    state_width = ssm_state.shape[1]
    dt_low = projected[:, :rank_width].astype(jnp.bfloat16)
    input_map = projected[:, rank_width : rank_width + state_width]
    output_map = projected[:, rank_width + state_width :]
    step_size = jax.nn.softplus(
        jnp.dot(dt_low, w_dt, preferred_element_type=jnp.float32) + dt_bias[None, :]
    )
    decay = jnp.exp(step_size[:, None, :] * (-jnp.exp(a_log))[None, :, :])
    new_state = decay * ssm_state + (step_size * activated)[:, None, :] * input_map[:, :, None]
    readout = jnp.sum(output_map[:, :, None] * new_state, axis=1) + skip_gain[None, :] * activated
    gated = (readout * jax.nn.silu(gate_branch)).astype(jnp.bfloat16)
    mamba_part = jnp.dot(gated, w_mamba_out, preferred_element_type=jnp.float32)
    share = sent_and_summed(mamba_part.astype(jnp.bfloat16), "seq", 1)
    share = taken_together(share, "head")
    hidden_out = (mid_stream.astype(jnp.float32) + share).astype(jnp.bfloat16)
    return (hidden_out, new_state)


def solution(mesh):
    in_specs = (
        P(("rep", "sub"), "seq"),
        P("seq"),
        P("seq", "head"),
        P("seq", "head"),
        P("seq", "head"),
        P("head", "seq"),
        P(("rep", "sub"), "head", "seq", None),
        P(("rep", "sub"), "head", "seq", None),
        P(("rep", "sub")),
        P(("rep", "sub")),
        P(),
        P(None, None, ("seq", "head")),
        P(None, ("seq", "head")),
        P(("seq", "head")),
        P(("rep", "sub"), None, ("seq", "head")),
        P(("seq", "head"), None),
        P(None, ("seq", "head")),
        P(("seq", "head")),
        P(None, ("seq", "head")),
        P(("seq", "head")),
        P(("rep", "sub"), None, ("seq", "head")),
        P(("seq", "head"), None),
    )
    out_specs = (P(("rep", "sub"), "seq"), P(("rep", "sub"), None, ("seq", "head")))
    return jax.shard_map(local, mesh=mesh, in_specs=in_specs, out_specs=out_specs, check_vma=False)
```

profile of v0, /device:TPU:80, one launch (start us, length us, event | category | flops | bytes accessed | tf_op | source)
XLA Modules:
  0.0 256.3 jit_solution(7575589292232890467)
XLA Ops:
  0.7 0.9 fusion.26
  1.6 1.1 convolution_bitcast_fusion
  2.8 0.1 convolution_bitcast_fusion.1
  2.9 0.7 copy-done.6
  3.6 0.1 convolution_bitcast_fusion.2
  3.7 1.0 broadcast_in_dim.31
  4.7 43.8 %all-to-all-start = ((f32[16,1,6152]{2,1,0:T(1,128)}), f32[16,1,6152]{2,1,0:T(1,128)S(1)}, u32[]{:S(2)}, u32[]{:S(2)}) async-start(f32[16,1,6152]{2,1,0:T(1,128)} %broadcast_in_dim.31), calls=%async_computation | async-start | bytes 802816 | tf_op jit(solution)/shard_map/all_to_all | solution.py:15
  48.6 0.1 multiply_cosine_fusion.1
  48.8 23.8 %all-to-all-done = f32[16,1,6152]{2,1,0:T(1,128)S(1)} async-done(((f32[16,1,6152]{2,1,0:T(1,128)}), f32[16,1,6152]{2,1,0:T(1,128)S(1)}, u32[]{:S(2)}, u32[]{:S(2)}) %all-to-all-start) | async-done | bytes 393760 | tf_op jit(solution)/shard_map/all_to_all | solution.py:15
  72.6 0.3 reduce_sum.82
  73.0 0.5 select_reduce_fusion
  73.6 0.2 fusion.11
  73.9 0.3 fusion
  74.2 0.8 broadcast_in_dim.34
  75.0 6.1 %all-to-all-start.1 = ((f32[16,34,128]{2,1,0:T(8,128)}), f32[16,34,128]{2,1,0:T(8,128)S(1)}, u32[]{:S(2)}, u32[]{:S(2)}) async-start(f32[16,34,128]{2,1,0:T(8,128)} %broadcast_in_dim.34), calls=%async_computation.1 | async-start | bytes 655360 | tf_op jit(solution)/shard_map/all_to_all | solution.py:15
  81.2 0.1 fusion.68
  81.4 0.2 fusion.51
  81.6 0.1 copy.143
  81.7 19.9 %all-to-all-done.1 = f32[16,34,128]{2,1,0:T(8,128)S(1)} async-done(((f32[16,34,128]{2,1,0:T(8,128)}), f32[16,34,128]{2,1,0:T(8,128)S(1)}, u32[]{:S(2)}, u32[]{:S(2)}) %all-to-all-start.1) | async-done | bytes 278560 | tf_op jit(solution)/shard_map/all_to_all | solution.py:15
  101.6 0.1 copy.148
  101.7 0.1 slice.141
  101.8 0.1 slice.142
  102.0 0.1 copy.153
  102.1 0.1 slice.162
  102.2 0.1 slice.163
  102.4 0.2 copy.147
  102.5 0.2 slice.138
  102.7 0.2 slice.143
  102.9 0.1 copy.149
  103.3 0.1 copy.131
  103.4 0.1 multiply_add_fusion
  103.6 0.2 slice.144
  103.8 0.2 slice.147
  104.1 0.1 copy.133
  104.2 0.1 copy.134
  104.3 0.1 multiply_add_fusion.2
  104.5 0.2 slice.148
  104.7 0.2 slice.151
  105.1 0.1 copy.135
  105.2 0.1 copy.136
  105.4 0.1 multiply_add_fusion.3
  105.5 0.2 fusion.22
  105.7 0.2 fusion.23
  105.9 15.5 %all_to_all.31 = f32[8,8,256]{2,1,0:T(8,128)S(1)} all-to-all(f32[8,8,256]{2,1,0:T(8,128)S(1)} %broadcast_in_dim.35), channel_id=1, replica_groups=mesh['rep'=2,'seq'=16,'head'=8,'sub'=2] {'head'}, dimensions={0} | all-to-all | bytes 131072 | tf_op jit(solution)/shard_map/all_to_all | solution.py:15
  121.4 0.6 broadcast_in_dim.36
  122.0 6.5 %all-to-all-start.3 = ((bf16[16,8,256]{2,1,0:T(8,128)(2,1)}), bf16[16,8,256]{2,1,0:T(8,128)(2,1)S(1)}, u32[]{:S(2)}, u32[]{:S(2)}) async-start(bf16[16,8,256]{2,1,0:T(8,128)(2,1)} %broadcast_in_dim.36), calls=%async_computation.3 | async-start | bytes 131072 | tf_op jit(solution)/shard_map/all_to_all | solution.py:15
  128.6 0.7 copy-done.13
  129.3 12.0 %all-to-all-done.3 = bf16[16,8,256]{2,1,0:T(8,128)(2,1)S(1)} async-done(((bf16[16,8,256]{2,1,0:T(8,128)(2,1)}), bf16[16,8,256]{2,1,0:T(8,128)(2,1)S(1)}, u32[]{:S(2)}, u32[]{:S(2)}) %all-to-all-start.3) | async-done | bytes 65568 | tf_op jit(solution)/shard_map/all_to_all | solution.py:15
  141.2 0.1 fusion.8
  141.4 0.1 fusion.10
  141.5 0.2 convolution_bitcast_fusion.3
  141.8 0.5 copy-done.11
  142.3 0.1 copy-done.8
  142.4 0.5 copy-done.14
  142.9 0.1 fusion.64
  143.0 54.0 %psum.14 = f32[8,288]{1,0:T(8,128)S(1)} all-reduce(f32[8,288]{1,0:T(8,128)S(1)} %fusion.64), channel_id=1, replica_groups=mesh['rep'=2,'seq'=16,'head'=8,'sub'=2] {'seq'}, use_global_device_ids=true, to_apply=%region_7.8 | all-reduce | flops 2304 | bytes 18432 | tf_op jit(solution)/shard_map/psum | solution.py:76
  197.1 27.5 %psum.15 = f32[8,288]{1,0:T(8,128)S(1)} all-reduce(f32[8,288]{1,0:T(8,128)S(1)} %psum.14), channel_id=1, replica_groups=mesh['rep'=2,'seq'=16,'head'=8,'sub'=2] {'head'}, use_global_device_ids=true, to_apply=%region_8.9 | all-reduce | flops 2304 | bytes 18432 | tf_op jit(solution)/shard_map/psum | solution.py:76
  224.6 0.1 fusion.79
  224.8 0.7 multiply_reduce_fusion
  225.5 0.7 copy-done.17
  226.2 0.6 convolution_convert_fusion
  226.7 17.0 %all_to_all.32 = bf16[16,8,256]{2,1,0:T(8,128)(2,1)S(1)} all-to-all(bf16[16,8,256]{2,1,0:T(8,128)(2,1)S(1)} %bitcast.133), channel_id=1, replica_groups=mesh['rep'=2,'seq'=16,'head'=8,'sub'=2] {'seq'}, dimensions={0} | all-to-all | bytes 131072 | tf_op jit(solution)/shard_map/all_to_all | solution.py:88
  243.7 11.9 %all_to_all.33 = f32[8,8,256]{2,1,0:T(8,128)S(1)} all-to-all(f32[8,8,256]{2,1,0:T(8,128)S(1)} %broadcast_in_dim.38), channel_id=1, replica_groups=mesh['rep'=2,'seq'=16,'head'=8,'sub'=2] {'head'}, dimensions={0} | all-to-all | bytes 131072 | tf_op jit(solution)/shard_map/all_to_all | solution.py:15
  255.7 0.6 add_convert_fusion.1
  (83 shorter events, 1.6 us)
Async XLA Ops:
  0.6 72.4 %copy-start = (bf16[8,1,512,128]{3,2,1,0:T(8,128)(2,1)S(1)}, bf16[8,1,512,128]{3,2,1,0:T(8,128)(2,1)}, u32[]{:S(2)}) copy-start(bf16[8,1,512,128]{3,2,1,0:T(8,128)(2,1)} %param.28) | copy-start | bytes 3145732
  0.6 0.9 copy-start.4
  1.6 1.2 copy-start.5
  1.6 1.2 copy-start.12
  2.7 0.8 copy-start.6
  4.7 43.8 %copy-start.20 = (s32[8]{0:T(128)S(1)}, s32[8]{0:T(128)}, u32[]{:S(2)}) copy-start(s32[8]{0:T(128)} %param.31) | copy-start | bytes 100
  4.7 43.9 %copy-start.18 = (s32[8]{0:T(128)S(1)}, s32[8]{0:T(128)}, u32[]{:S(2)}) copy-start(s32[8]{0:T(128)} %param.30) | copy-start | bytes 100
  4.7 67.9 %all-to-all-start = ((f32[16,1,6152]{2,1,0:T(1,128)}), f32[16,1,6152]{2,1,0:T(1,128)S(1)}, u32[]{:S(2)}, u32[]{:S(2)}) async-start(f32[16,1,6152]{2,1,0:T(1,128)} %broadcast_in_dim.31), calls=%async_computation | async-start | bytes 802816 | tf_op jit(solution)/shard_map/all_to_all | solution.py:15
  48.5 25.4 %copy-start.1 = (bf16[8,1,512,128]{3,2,1,0:T(8,128)(2,1)S(1)}, bf16[8,1,512,128]{3,2,1,0:T(8,128)(2,1)}, u32[]{:S(2)}) copy-start(bf16[8,1,512,128]{3,2,1,0:T(8,128)(2,1)} %param.29) | copy-start | bytes 3145732
  75.0 26.6 %all-to-all-start.1 = ((f32[16,34,128]{2,1,0:T(8,128)}), f32[16,34,128]{2,1,0:T(8,128)S(1)}, u32[]{:S(2)}, u32[]{:S(2)}) async-start(f32[16,34,128]{2,1,0:T(8,128)} %broadcast_in_dim.34), calls=%async_computation.1 | async-start | bytes 655360 | tf_op jit(solution)/shard_map/all_to_all | solution.py:15
  103.6 2.1 copy-start.19
  103.8 37.7 %copy-start.2 = (bf16[2,4096,64]{1,2,0:T(8,128)(2,1)S(1)}, bf16[2,4096,64]{1,2,0:T(8,128)(2,1)}, u32[]{:S(2)}) copy-start(bf16[2,4096,64]{1,2,0:T(8,128)(2,1)} %param.33) | copy-start | bytes 3145732
  122.0 6.5 %copy-start.10 = (f32[4096]{0:T(1024)S(1)}, f32[4096]{0:T(1024)}, u32[]{:S(2)}) copy-start(f32[4096]{0:T(1024)} %param.32) | copy-start | bytes 49156
  122.0 19.2 %all-to-all-start.3 = ((bf16[16,8,256]{2,1,0:T(8,128)(2,1)}), bf16[16,8,256]{2,1,0:T(8,128)(2,1)S(1)}, u32[]{:S(2)}, u32[]{:S(2)}) async-start(bf16[16,8,256]{2,1,0:T(8,128)(2,1)} %broadcast_in_dim.36), calls=%async_computation.3 | async-start | bytes 131072 | tf_op jit(solution)/shard_map/all_to_all | solution.py:15
  128.6 0.7 copy-start.13
  141.4 84.1 %copy-start.3 = (bf16[64,4096]{1,0:T(8,128)(2,1)S(1)}, bf16[64,4096]{1,0:T(8,128)(2,1)}, u32[]{:S(2)}) copy-start(bf16[64,4096]{1,0:T(8,128)(2,1)} %param.43) | copy-start | bytes 1572868
  141.5 0.8 copy-start.11
  141.5 0.8 copy-start.15
  141.5 0.9 copy-start.8
  142.3 0.7 copy-start.14
  142.3 82.4 %copy-start.16 = (f32[64]{0:T(128)S(1)}, f32[64]{0:T(128)}, u32[]{:S(2)}) copy-start(f32[64]{0:T(128)} %param.39) | copy-start | bytes 772
  142.9 81.7 %copy-start.9 = (bf16[256,64]{0,1:T(8,128)(2,1)S(1)}, bf16[256,64]{0,1:T(8,128)(2,1)}, u32[]{:S(2)}) copy-start(bf16[256,64]{0,1:T(8,128)(2,1)} %param.38) | copy-start | bytes 98308
  143.0 81.7 %copy-start.7 = (f32[8,16,64]{2,1,0:T(8,128)S(1)}, f32[8,16,64]{2,1,0:T(8,128)}, u32[]{:S(2)}) copy-start(f32[8,16,64]{2,1,0:T(8,128)} %param.42) | copy-start | bytes 98308
  225.5 0.7 copy-start.17
where the time goes:
time: 257 us; the launch traced here: 256 us
  blocking collectives  126 us (49%)
  starting transfers between devices  56.5 us (22%)
  waiting for transfers between devices  55.7 us (22%)
  local copies, waits for them, and re-layouts  9.12 us (4%)
  other arithmetic  4.35 us (2%)
  matrix products  3.63 us (1%)
    psum x2, blocking collectives, over_axes(): value = lax.psum(value, axis)  81.5 us
    all_to_all x3, starting transfers between devices, copy_for_each(): lax.all_to_all(jnp.broadcast_to(value[None], (peers, *value.shape)), axis...  56.5 us
    all_to_all x3, waiting for transfers between devices, copy_for_each(): lax.all_to_all(jnp.broadcast_to(value[None], (peers, *value.shape)), axis...  55.7 us
    all_to_all x2, blocking collectives, copy_for_each(): lax.all_to_all(jnp.broadcast_to(value[None], (peers, *value.shape)), axis...  27.4 us
    all_to_all x1, blocking collectives, sent_and_summed(): lax.all_to_all(in_blocks(value, dim, peers), axis, 0, 0, tiled=True)  17 us
  transfers between devices with their start and end apart: 3, of which 3 were waited for; matrix products, arithmetic and copies ran while one was open for 0% of the time, Pallas kernels for 0%

commit v1 on v0

v1 whole, which is shorter than its diff:
```python
import functools
import math

import jax
import jax.numpy as jnp
import numpy as np
from jax import lax
from jax.experimental import pallas as pl
from jax.experimental.pallas import tpu as pltpu
from jax.sharding import PartitionSpec as P

NORM_EPS = 1e-05
FLOOR = -1e30
ROPE_BASE = 10000.0
MESH = pl.DeviceIdType.MESH
F32 = jnp.float32
BF16 = jnp.bfloat16


def far_first(n):
    return sorted(range(1, n), key=lambda k: -min(k, n - k))


def near_first(n):
    return far_first(n)[::-1]


def dot(a, b):
    return lax.dot_general(a, b, (((1,), (0,)), ((), ())), preferred_element_type=F32)


def dot_t(a, b):
    return lax.dot_general(a, b, (((1,), (1,)), ((), ())), preferred_element_type=F32)


def diagonal(shape):
    return lax.broadcasted_iota(jnp.int32, shape, 0) == lax.broadcasted_iota(jnp.int32, shape, 1)


def column_to_row(column):
    rows = column.shape[0]
    spread = jnp.where(diagonal((rows, 128)), jnp.broadcast_to(column, (rows, 128)), 0.0)
    return jnp.sum(spread, axis=0, keepdims=True)


def row_to_column(row, rows):
    spread = jnp.where(diagonal((rows, row.shape[1])), jnp.broadcast_to(row, (rows, row.shape[1])), 0.0)
    return jnp.sum(spread, axis=1, keepdims=True)


def send_all(axis, n, buffer, send_sem, recv_sem):
    me = lax.axis_index(axis)
    for k in far_first(n):
        pltpu.make_async_remote_copy(
            src_ref=buffer.at[0],
            dst_ref=buffer.at[k],
            send_sem=send_sem,
            recv_sem=recv_sem(k) if callable(recv_sem) else recv_sem,
            device_id={axis: lax.rem(me + k, n)},
            device_id_type=MESH,
        ).start()


def wait_for(buffer, sem, slots):
    part = buffer.at[pl.ds(0, slots)]
    pltpu.make_async_copy(part, part, sem).wait()


def kernel(nz, nx, *refs):
    (
        tokens_h, attn_gain_h, w_query_h, w_key_h, w_value_h, w_out_h, keys_h, values_h, lengths_h, positions_h,
        mamba_gain_h, w_in_h, conv_weight_h, conv_bias_h, conv_state_h, w_xproj_h, w_dt_h, dt_bias_h, a_log_h,
        skip_gain_h, ssm_h, w_mout_h, freq_h,
        hidden_o, state_o,
        tokens, attn_gain, w_query, w_key, w_value, w_out, keys, values, lengths, positions,
        mamba_gain, w_in, conv_weight, conv_bias, conv_state, w_xproj, w_dt, dt_bias, a_log,
        skip_gain, ssm, w_mout, freq,
        load_sem,
        q_buf, below, up_to, total_q, kv_buf, knew, vnew, acc_buf, aux_buf, part_buf, mid_buf, px_buf, pz_buf,
        out_src, share_buf, fin_buf,
        s_q, r_q, s_up, r_up, go, s_kv, r_kv, s_acc, r_acc, s_aux, r_aux, s_part, r_part, s_mid, r_mid,
        s_px, r_px, s_pz, r_pz, s_sh, r_sh, s_fin, r_fin,
    ) = refs
    z = lax.axis_index("seq")
    x = lax.axis_index("head")
    is_owner = z == 0

    loads = {}
    pairs = dict(
        tokens=(tokens_h, tokens), attn_gain=(attn_gain_h, attn_gain), w_query=(w_query_h, w_query), w_key=(w_key_h, w_key),
        w_value=(w_value_h, w_value), positions=(positions_h, positions), freq=(freq_h, freq), lengths=(lengths_h, lengths),
        keys=(keys_h, keys), values=(values_h, values), w_out=(w_out_h, w_out), mamba_gain=(mamba_gain_h, mamba_gain),
        w_in=(w_in_h, w_in), conv_weight=(conv_weight_h, conv_weight), conv_bias=(conv_bias_h, conv_bias),
        conv_state=(conv_state_h, conv_state), w_xproj=(w_xproj_h, w_xproj), w_dt=(w_dt_h, w_dt), dt_bias=(dt_bias_h, dt_bias),
        a_log=(a_log_h, a_log), skip_gain=(skip_gain_h, skip_gain), ssm=(ssm_h, ssm), w_mout=(w_mout_h, w_mout),
    )
    for i, (name, (source, target)) in enumerate(pairs.items()):
        loads[name] = pltpu.make_async_copy(source, target, load_sem.at[i])
        loads[name].start()

    def need(*names):
        for name in names:
            loads.pop(name).wait()

    barrier = pltpu.get_barrier_semaphore()
    for k in far_first(nx):
        pl.semaphore_signal(barrier, inc=1, device_id={"head": lax.rem(x + k, nx)}, device_id_type=MESH)
    pl.semaphore_wait(barrier, nx - 1 + jnp.minimum(z, 1))

    @pl.when(z > 0)
    def _():
        pl.semaphore_signal(go, inc=1, device_id={"seq": z - 1}, device_id_type=MESH)

    @pl.when(z < nz - 1)
    def _():
        pl.semaphore_signal(barrier, inc=1, device_id={"seq": z + 1}, device_id_type=MESH)

    rows = tokens.shape[0]
    feats = tokens.shape[1]
    hd = keys.shape[2]
    span = keys.shape[1]
    groups = w_query.shape[1] // hd
    qrows = groups * rows
    width = feats * nz
    chans = w_xproj.shape[0]
    rank = w_dt.shape[1]
    nstate = a_log.shape[0]

    need("tokens", "attn_gain", "w_query")
    token_f = tokens[...].astype(F32)
    lifted = (token_f * attn_gain[...]).astype(BF16)
    qw = w_query.shape[1]
    q_buf[0, :, :qw] = dot(lifted, w_query[...])
    q_buf[0, :, qw:] = jnp.broadcast_to(jnp.sum(token_f * token_f, axis=1, keepdims=True), (rows, 128))

    for k in far_first(nz):

        @pl.when(z >= k)
        def _(k=k):
            pltpu.make_async_remote_copy(
                src_ref=q_buf.at[0], dst_ref=q_buf.at[k], send_sem=s_q.at[k], recv_sem=r_q.at[k],
                device_id={"seq": z - k}, device_id_type=MESH,
            ).start()

    need("w_key", "w_value")
    kv_buf[0, :, :hd] = dot(lifted, w_key[...])
    kv_buf[0, :, hd:] = dot(lifted, w_value[...])

    @pl.when(z > 0)
    def _():
        pltpu.make_async_remote_copy(
            src_ref=kv_buf.at[0], dst_ref=kv_buf.at[z], send_sem=s_kv, recv_sem=r_kv,
            device_id={"seq": 0}, device_id_type=MESH,
        ).start()

    knew[...] = jnp.zeros_like(knew)
    vnew[...] = jnp.zeros_like(vnew)
    need("positions", "freq", "lengths")
    angle = row_to_column(positions[...].astype(F32), rows) * freq[...]
    cosine = jnp.cos(angle)
    sine = jnp.sin(angle)
    cosine = jnp.concatenate([cosine, cosine], axis=1)
    sine = jnp.concatenate([-sine, sine], axis=1)

    def rotated(v):
        return v * cosine + pltpu.roll(v, hd // 2, 1) * sine

    limit = row_to_column(lengths[...].astype(F32), rows)
    limit = jnp.concatenate([limit] * groups, axis=0)
    spot = (lax.broadcasted_iota(jnp.int32, (qrows, span), 1) + z * span).astype(F32)
    live = spot < limit
    row_of = lax.broadcasted_iota(jnp.int32, (qrows, hd), 0) % rows
    row_of_wide = lax.broadcasted_iota(jnp.int32, (qrows, span), 0) % rows

    up_to[...] = q_buf[0]

    @pl.when(z > 0)
    def _():
        pltpu.make_async_copy(below, below, r_up).wait()
        up_to[...] = q_buf[0] + below[...]

    total_q[...] = up_to[...]

    @pl.when(z < nz - 1)
    def _():
        pl.semaphore_wait(go, 1)
        pltpu.make_async_remote_copy(
            src_ref=up_to, dst_ref=below, send_sem=s_up, recv_sem=r_up, device_id={"seq": z + 1}, device_id_type=MESH,
        ).start()

    for k in range(1, nz):

        @pl.when(z + k < nz)
        def _(k=k):
            pltpu.make_async_copy(q_buf.at[k], q_buf.at[k], r_q.at[k]).wait()
            total_q[...] += q_buf[k]

    r_a = lax.rsqrt(total_q[:, qw:] / width + NORM_EPS)

    @pl.when(is_owner)
    def _():
        wait_for(kv_buf, r_kv, nz - 1)
        kv = kv_buf[0]
        for k in range(1, nz):
            kv = kv + kv_buf[k]
        knew[...] = rotated(kv[:, :hd] * r_a).astype(BF16).astype(F32)
        vnew[...] = (kv[:, hd:] * r_a).astype(BF16).astype(F32)

    q = [rotated(total_q[:, g * hd : (g + 1) * hd] * r_a) for g in range(groups)]
    q = jnp.concatenate(q, axis=0).astype(BF16)

    need("keys")
    scores = jnp.zeros((qrows, span), F32)
    for b in range(rows):
        scores = jnp.where(row_of_wide == b, dot_t(q, keys[b]), scores)
    scale = hd ** (-0.5)
    scores = scores * scale
    top = jnp.max(jnp.where(live, scores, FLOOR), axis=1, keepdims=True)
    fresh = jnp.sum(q.astype(F32) * jnp.concatenate([knew[...]] * groups, axis=0), axis=1, keepdims=True) * scale
    mine = jnp.broadcast_to(is_owner, fresh.shape)
    top = jnp.maximum(top, jnp.where(mine, fresh, FLOOR))
    weights = jnp.where(live, jnp.exp(scores - top), 0.0)
    new_weight = jnp.where(mine, jnp.exp(fresh - top), 0.0)
    total = jnp.sum(weights, axis=1, keepdims=True) + new_weight
    weights = weights.astype(BF16)
    need("values")
    acc = jnp.zeros((qrows, hd), F32)
    for b in range(rows):
        acc = jnp.where(row_of == b, dot(weights, values[b]), acc)
    acc = acc + new_weight * jnp.concatenate([vnew[...]] * groups, axis=0)
    acc_buf[0] = acc.astype(BF16)
    aux_buf[0] = column_to_row(top) + pltpu.roll(column_to_row(total), 64, 1)
    send_all("seq", nz, aux_buf, s_aux, r_aux)
    send_all("seq", nz, acc_buf, s_acc, r_acc)

    need("w_out")
    wait_for(aux_buf, r_aux, nz - 1)
    aux = jnp.concatenate([aux_buf[k] for k in range(nz)], axis=0)
    factor = jnp.exp(aux - jnp.max(aux, axis=0, keepdims=True))
    whole = jnp.sum(factor * pltpu.roll(aux, 64, 1), axis=0, keepdims=True)
    lane = lax.broadcasted_iota(jnp.int32, (nz, 128), 1)
    share = jnp.where(lane < qrows, factor / whole, 0.0)
    share = jnp.concatenate([share, jnp.zeros((128 - nz, 128), F32)], axis=0).T
    wait_for(acc_buf, r_acc, nz - 1)
    attended = share[:qrows, 0:1] * acc_buf[0].astype(F32)
    for k in range(1, nz):
        attended = attended + share[:qrows, k : k + 1] * acc_buf[k].astype(F32)
    attended = jnp.concatenate([attended[g * rows : (g + 1) * rows] for g in range(groups)], axis=1).astype(BF16)
    part_buf[0] = dot(attended, w_out[...]).astype(BF16)
    send_all("head", nx, part_buf, s_part, r_part)
    need("mamba_gain", "w_in")
    wait_for(part_buf, r_part, nx - 1)
    summed = part_buf[lax.rem(x, nx)].astype(F32)
    for j in range(1, nx):
        summed = summed + part_buf[lax.rem(x - j + nx, nx)].astype(F32)
    mid = (token_f + summed).astype(BF16)
    mid_buf[0] = mid
    circle = sorted(range(1, nz), key=lambda k: min(k, nz - k))
    ends = (0, nz // 2, max(nz // 2, nz - 4), nz - 1)
    rings = [circle[i:j] for i, j in zip(ends, ends[1:]) if j > i]
    ring_of = {k: i for i, r in enumerate(rings) for k in r}
    send_all("seq", nz, mid_buf, s_mid, lambda k: r_mid.at[ring_of[k]])

    def block_of(k):
        at = pl.multiple_of(lax.rem(z - k + nz, nz) * feats, feats)
        block = mid_buf[k].astype(F32)
        raised = (block * mamba_gain[:, pl.ds(at, feats)]).astype(BF16)
        return block * block, dot_t(raised, w_in[:, pl.ds(at, feats)])

    squares, both = block_of(0)
    for i, ring in enumerate(rings):
        wait_for(mid_buf, r_mid.at[i], len(ring))
        for k in ring:
            more, extra = block_of(k)
            squares = squares + more
            both = both + extra
    both = both * lax.rsqrt(jnp.sum(squares, axis=1, keepdims=True) / width + NORM_EPS)
    inner = both[:, :chans]
    gate = both[:, chans:]

    need("conv_weight", "conv_bias", "conv_state", "w_xproj")
    mixed = inner * conv_weight[3:4, :] + conv_bias[...]
    for k in range(3):
        mixed = mixed + conv_state[k] * conv_weight[k : k + 1, :]
    u = mixed / (1.0 + jnp.exp(-mixed))
    proj = dot(u.astype(BF16), w_xproj[...])
    px_buf[0] = jnp.concatenate([proj, jnp.zeros((rows, px_buf.shape[2] - proj.shape[1]), F32)], axis=1).astype(BF16)
    send_all("head", nx, px_buf, s_px, r_px)
    need("w_dt", "dt_bias", "a_log", "skip_gain", "ssm", "w_mout")
    decay_rate = -jnp.exp(a_log[...])
    gated = gate / (1.0 + jnp.exp(-gate))
    wait_for(px_buf, r_px, nx - 1)
    proj = px_buf[0].astype(F32)
    for k in range(1, nx):
        proj = proj + px_buf[k].astype(F32)
    pz_buf[0] = proj.astype(BF16)
    send_all("seq", nz, pz_buf, s_pz, r_pz)
    wait_for(pz_buf, r_pz, nz - 1)
    proj = pz_buf[0].astype(F32)
    for k in range(1, nz):
        proj = proj + pz_buf[k].astype(F32)

    pre = dot_t(proj[:, :rank].astype(BF16), w_dt[...]) + dt_bias[...]
    step = jnp.maximum(pre, 0.0) + jnp.log(1.0 + jnp.exp(-jnp.abs(pre)))
    maps = jnp.concatenate([proj[:, rank : rank + 128], jnp.zeros((128 - rows, 128), F32)], axis=0).T
    drive = step * u
    reads = []
    for b in range(rows):
        state = (
            jnp.exp(step[b : b + 1, :] * decay_rate) * ssm[b]
            + drive[b : b + 1, :] * maps[:nstate, b : b + 1]
        )
        state_o[b] = state
        reads.append(jnp.sum(maps[nstate : 2 * nstate, b : b + 1] * state, axis=0, keepdims=True))
    y = (jnp.concatenate(reads, axis=0) + skip_gain[...] * u) * gated
    y = y.astype(BF16)

    def out_block(k):
        at = pl.multiple_of(lax.rem(z + k, nz) * feats, feats)
        return dot(y, w_mout[:, pl.ds(at, feats)]).astype(BF16)

    for k in far_first(nz):
        out_src[k] = out_block(k)
        pltpu.make_async_remote_copy(
            src_ref=out_src.at[k], dst_ref=share_buf.at[k], send_sem=s_sh, recv_sem=r_sh,
            device_id={"seq": lax.rem(z + k, nz)}, device_id_type=MESH,
        ).start()
    result = out_block(0).astype(F32)
    wait_for(share_buf, r_sh, nz - 1)
    for k in range(1, nz):
        result = result + share_buf[k].astype(F32)
    fin_buf[0] = result
    send_all("head", nx, fin_buf, s_fin, r_fin)

    for k in range(1, nz):

        @pl.when(z >= k)
        def _(k=k):
            pltpu.make_async_copy(q_buf.at[0], q_buf.at[0], s_q.at[k]).wait()

    @pl.when(z > 0)
    def _():
        pltpu.make_async_copy(kv_buf.at[0], kv_buf.at[0], s_kv).wait()

    @pl.when(z < nz - 1)
    def _():
        pltpu.make_async_copy(up_to, up_to, s_up).wait()

    wait_for(aux_buf, s_aux, nz - 1)
    wait_for(acc_buf, s_acc, nz - 1)
    wait_for(part_buf, s_part, nx - 1)
    wait_for(mid_buf, s_mid, nz - 1)
    wait_for(px_buf, s_px, nx - 1)
    wait_for(pz_buf, s_pz, nz - 1)
    wait_for(share_buf, s_sh, nz - 1)
    wait_for(fin_buf, r_fin, nx - 1)
    result = fin_buf[lax.rem(x, nx)]
    for j in range(1, nx):
        result = result + fin_buf[lax.rem(x - j + nx, nx)]
    hidden_o[...] = (mid.astype(F32) + result).astype(BF16)
    wait_for(fin_buf, s_fin, nx - 1)


def put_out(hidden, state, hidden_o, state_o, sem):
    copies = [pltpu.make_async_copy(hidden, hidden_o, sem.at[0]), pltpu.make_async_copy(state, state_o, sem.at[1])]
    for copy in copies:
        copy.start()
    for copy in copies:
        copy.wait()


def local(nz, nx, *args):
    (
        tokens, attn_gain, w_query, w_key, w_value, w_out, keys, values, lengths, positions, mamba_gain, w_in,
        conv_weight, conv_bias, conv_state, w_xproj, w_dt, dt_bias, a_log, skip_gain, ssm, w_mout,
    ) = args
    rows, feats = tokens.shape
    hd = keys.shape[3]
    span = keys.shape[2]
    half = hd // 2
    qrows = w_query.shape[1] // hd * rows
    two, width, chans = w_in.shape
    freq = jnp.asarray(np.exp(-math.log(ROPE_BASE) * 2.0 * np.arange(half) / (2 * half)).reshape(1, half), F32)
    operands = (
        tokens, attn_gain.reshape(1, -1), w_query, w_key, w_value, w_out,
        keys.reshape(rows, span, hd), values.reshape(rows, span, hd), lengths.reshape(1, -1), positions.reshape(1, -1),
        mamba_gain.reshape(1, -1), jnp.transpose(w_in, (0, 2, 1)).reshape(two * chans, width),
        conv_weight, conv_bias.reshape(1, -1), jnp.transpose(conv_state, (1, 0, 2)), w_xproj,
        jnp.transpose(w_dt), dt_bias.reshape(1, -1), a_log, skip_gain.reshape(1, -1), ssm, w_mout, freq,
    )
    pad = -(-w_xproj.shape[1] // 128) * 128
    dma = pltpu.SemaphoreType.DMA
    buffers = [
        ((nz, rows, w_query.shape[1] + 128), F32),
        ((rows, w_query.shape[1] + 128), F32),
        ((rows, w_query.shape[1] + 128), F32),
        ((rows, w_query.shape[1] + 128), F32),
        ((nz, rows, 2 * hd), F32),
        ((rows, hd), F32),
        ((rows, hd), F32),
        ((nz, qrows, hd), BF16),
        ((nz, 1, 128), F32),
        ((nx, rows, feats), BF16),
        ((nz, rows, feats), BF16),
        ((nx, rows, pad), BF16),
        ((nz, rows, pad), BF16),
        ((nz, rows, feats), BF16),
        ((nz, rows, feats), BF16),
        ((nx, rows, feats), F32),
    ]
    sems = [dma((nz,)), dma((nz,)), dma, dma, pltpu.SemaphoreType.REGULAR] + [dma] * 8 + [dma, dma((3,))] + [dma] * 8
    hidden, state = pl.pallas_call(
        functools.partial(kernel, nz, nx),
        out_shape=(
            pltpu.VMEM((rows, feats), BF16),
            pltpu.VMEM(ssm.shape, F32),
        ),
        in_specs=[pl.BlockSpec(memory_space=pltpu.HBM)] * len(operands),
        out_specs=(pl.BlockSpec(memory_space=pltpu.VMEM), pl.BlockSpec(memory_space=pltpu.VMEM)),
        scratch_shapes=[pltpu.VMEM(o.shape, o.dtype) for o in operands]
        + [dma((len(operands),))]
        + [pltpu.VMEM(shape, kind) for shape, kind in buffers]
        + sems,
        compiler_params=pltpu.CompilerParams(
            collective_id=0, has_side_effects=True, vmem_limit_bytes=48 * 2**20
        ),
        name="decode_step",
    )(*[pltpu.with_memory_space_constraint(o, pltpu.HBM) for o in operands])
    return pl.pallas_call(
        put_out,
        out_shape=(jax.ShapeDtypeStruct((rows, feats), BF16), jax.ShapeDtypeStruct(ssm.shape, F32)),
        in_specs=[pl.BlockSpec(memory_space=pltpu.VMEM)] * 2,
        out_specs=(pl.BlockSpec(memory_space=pltpu.HBM), pl.BlockSpec(memory_space=pltpu.HBM)),
        scratch_shapes=[dma((2,))],
        name="put_out",
        compiler_params=pltpu.CompilerParams(vmem_limit_bytes=2**20),
    )(*[pltpu.with_memory_space_constraint(o, pltpu.VMEM) for o in (hidden, state)])


def solution(mesh):
    batch = ("rep", "sub")
    chan = ("seq", "head")
    in_specs = (
        P(batch, "seq"), P("seq"), P("seq", "head"), P("seq", "head"), P("seq", "head"), P("head", "seq"),
        P(batch, "head", "seq", None), P(batch, "head", "seq", None), P(batch), P(batch), P(), P(None, None, chan),
        P(None, chan), P(chan), P(batch, None, chan), P(chan, None), P(None, chan), P(chan), P(None, chan), P(chan),
        P(batch, None, chan), P(chan, None),
    )
    out_specs = (P(batch, "seq"), P(batch, None, chan))
    body = functools.partial(local, mesh.shape["seq"], mesh.shape["head"])
    return jax.shard_map(body, mesh=mesh, in_specs=in_specs, out_specs=out_specs, check_vma=False)
```

time: 257 us -> 138 us (0.54)
  the two profiles are of different devices: /device:TPU:80 before, /device:TPU:66 now
where the time goes in v1:
time: 138 us
  Pallas kernels  137 us (99%)
    pallas_call x1, Pallas kernels, local(): pl.pallas_call(functools.partial(kernel, nz, nx), out_shape=(pltpu.VMEM((...  137 us

profile of v1, /device:TPU:66, one launch (start us, length us, event | category | flops | bytes accessed | tf_op | source)
XLA Modules:
  0.0 138.1 jit_solution(10651665327671807694)
XLA Ops:
  0.6 136.8 %decode_step.1 = (bf16[8,256]{1,0:T(8,128)(2,1)S(1)}, f32[8,16,64]{2,1,0:T(8,128)S(1)}) custom-call(bf16[8,256]{1,0:T(8,128)(2,1)} %refs_0_.1, f32[1,256]{1,0:T(1,128)} %bitcast.20, bf16[256,512]{1,0:T(8,128)(2,1)} %refs_2_.1, bf16[256,128]{1,0:T(8,128)(2,1)} %refs_3_.1, bf16[256,128]{1,0:T(8,128)(2,1)} %refs_4_.1, bf16[512,256]{1,0:T(8,128)(2,1)} %refs_5_.1, ...), custom_call_target="tpu_custom_call" | custom-call | tf_op jit(solution)/shard_map/decode_step/pallas_call | solution.py:412
  137.5 0.7 put_out.1

commit v2 on v1

--- a/solution.py
+++ b/solution.py
@@ -83,7 +83,9 @@
     ) = refs
     z = lax.axis_index("seq")
     x = lax.axis_index("head")
-    is_owner = z == 0
+    place = lax.rem(z + nz - 1, nz)
+    down, up = lax.rem(z + nz - 1, nz), lax.rem(z + 1, nz)
+    is_owner = place == 0
 
     loads = {}
     pairs = dict(
@@ -105,15 +107,15 @@
     barrier = pltpu.get_barrier_semaphore()
     for k in far_first(nx):
         pl.semaphore_signal(barrier, inc=1, device_id={"head": lax.rem(x + k, nx)}, device_id_type=MESH)
-    pl.semaphore_wait(barrier, nx - 1 + jnp.minimum(z, 1))
-
-    @pl.when(z > 0)
-    def _():
-        pl.semaphore_signal(go, inc=1, device_id={"seq": z - 1}, device_id_type=MESH)
-
-    @pl.when(z < nz - 1)
-    def _():
-        pl.semaphore_signal(barrier, inc=1, device_id={"seq": z + 1}, device_id_type=MESH)
+    pl.semaphore_wait(barrier, nx - 1 + jnp.minimum(place, 1))
+
+    @pl.when(place > 0)
+    def _():
+        pl.semaphore_signal(go, inc=1, device_id={"seq": down}, device_id_type=MESH)
+
+    @pl.when(place < nz - 1)
+    def _():
+        pl.semaphore_signal(barrier, inc=1, device_id={"seq": up}, device_id_type=MESH)
 
     rows = tokens.shape[0]
     feats = tokens.shape[1]
@@ -135,22 +137,22 @@
 
     for k in far_first(nz):
 
-        @pl.when(z >= k)
+        @pl.when(place >= k)
         def _(k=k):
             pltpu.make_async_remote_copy(
                 src_ref=q_buf.at[0], dst_ref=q_buf.at[k], send_sem=s_q.at[k], recv_sem=r_q.at[k],
-                device_id={"seq": z - k}, device_id_type=MESH,
+                device_id={"seq": lax.rem(z + nz - k, nz)}, device_id_type=MESH,
             ).start()
 
     need("w_key", "w_value")
     kv_buf[0, :, :hd] = dot(lifted, w_key[...])
     kv_buf[0, :, hd:] = dot(lifted, w_value[...])
 
-    @pl.when(z > 0)
+    @pl.when(place > 0)
     def _():
         pltpu.make_async_remote_copy(
-            src_ref=kv_buf.at[0], dst_ref=kv_buf.at[z], send_sem=s_kv, recv_sem=r_kv,
-            device_id={"seq": 0}, device_id_type=MESH,
+            src_ref=kv_buf.at[0], dst_ref=kv_buf.at[place], send_sem=s_kv, recv_sem=r_kv,
+            device_id={"seq": 1}, device_id_type=MESH,
         ).start()
 
     knew[...] = jnp.zeros_like(knew)
@@ -174,23 +176,23 @@
 
     up_to[...] = q_buf[0]
 
-    @pl.when(z > 0)
+    @pl.when(place > 0)
     def _():
         pltpu.make_async_copy(below, below, r_up).wait()
         up_to[...] = q_buf[0] + below[...]
 
     total_q[...] = up_to[...]
 
-    @pl.when(z < nz - 1)
+    @pl.when(place < nz - 1)
     def _():
         pl.semaphore_wait(go, 1)
         pltpu.make_async_remote_copy(
-            src_ref=up_to, dst_ref=below, send_sem=s_up, recv_sem=r_up, device_id={"seq": z + 1}, device_id_type=MESH,
+            src_ref=up_to, dst_ref=below, send_sem=s_up, recv_sem=r_up, device_id={"seq": up}, device_id_type=MESH,
         ).start()
 
     for k in range(1, nz):
 
-        @pl.when(z + k < nz)
+        @pl.when(place + k < nz)
         def _(k=k):
             pltpu.make_async_copy(q_buf.at[k], q_buf.at[k], r_q.at[k]).wait()
             total_q[...] += q_buf[k]
@@ -334,15 +336,15 @@
 
     for k in range(1, nz):
 
-        @pl.when(z >= k)
+        @pl.when(place >= k)
         def _(k=k):
             pltpu.make_async_copy(q_buf.at[0], q_buf.at[0], s_q.at[k]).wait()
 
-    @pl.when(z > 0)
+    @pl.when(place > 0)
     def _():
         pltpu.make_async_copy(kv_buf.at[0], kv_buf.at[0], s_kv).wait()
 
-    @pl.when(z < nz - 1)
+    @pl.when(place < nz - 1)
     def _():
         pltpu.make_async_copy(up_to, up_to, s_up).wait()
 

time: 138 us -> 108 us (0.78)
  the two profiles are of different devices: /device:TPU:66 before, /device:TPU:80 now
where the time goes in v2:
time: 108 us
  Pallas kernels  107 us (99%)
    pallas_call x1, Pallas kernels, local(): pl.pallas_call(functools.partial(kernel, nz, nx), out_shape=(pltpu.VMEM((...  106 us

profile of v2, /device:TPU:80, one launch (start us, length us, event | category | flops | bytes accessed | tf_op | source)
XLA Modules:
  0.0 107.5 jit_solution(5871683487526276232)
XLA Ops:
  0.6 106.2 %decode_step.1 = (bf16[8,256]{1,0:T(8,128)(2,1)S(1)}, f32[8,16,64]{2,1,0:T(8,128)S(1)}) custom-call(bf16[8,256]{1,0:T(8,128)(2,1)} %refs_0_.1, f32[1,256]{1,0:T(1,128)} %bitcast.20, bf16[256,512]{1,0:T(8,128)(2,1)} %refs_2_.1, bf16[256,128]{1,0:T(8,128)(2,1)} %refs_3_.1, bf16[256,128]{1,0:T(8,128)(2,1)} %refs_4_.1, bf16[512,256]{1,0:T(8,128)(2,1)} %refs_5_.1, ...), custom_call_target="tpu_custom_call" | custom-call | tf_op jit(solution)/shard_map/decode_step/pallas_call | solution.py:414
  106.9 0.7 put_out.1

commit v3 on v2

--- a/solution.py
+++ b/solution.py
@@ -78,13 +78,13 @@
         load_sem,
         q_buf, below, up_to, total_q, kv_buf, knew, vnew, acc_buf, aux_buf, part_buf, mid_buf, px_buf, pz_buf,
         out_src, share_buf, fin_buf,
-        s_q, r_q, s_up, r_up, go, s_kv, r_kv, s_acc, r_acc, s_aux, r_aux, s_part, r_part, s_mid, r_mid,
+        s_q, r_q, s_up, r_up, go, ready_x, ready, s_kv, r_kv, s_acc, r_acc, s_aux, r_aux, s_part, r_part, s_mid, r_mid,
         s_px, r_px, s_pz, r_pz, s_sh, r_sh, s_fin, r_fin,
     ) = refs
     z = lax.axis_index("seq")
     x = lax.axis_index("head")
     place = lax.rem(z + nz - 1, nz)
-    down, up = lax.rem(z + nz - 1, nz), lax.rem(z + 1, nz)
+    up = lax.rem(z + 1, nz)
     is_owner = place == 0
 
     loads = {}
@@ -105,17 +105,23 @@
             loads.pop(name).wait()
 
     barrier = pltpu.get_barrier_semaphore()
-    for k in far_first(nx):
-        pl.semaphore_signal(barrier, inc=1, device_id={"head": lax.rem(x + k, nx)}, device_id_type=MESH)
-    pl.semaphore_wait(barrier, nx - 1 + jnp.minimum(place, 1))
-
-    @pl.when(place > 0)
-    def _():
-        pl.semaphore_signal(go, inc=1, device_id={"seq": down}, device_id_type=MESH)
+
+    @pl.when(place == 0)
+    def _():
+        for k in far_first(nx):
+            pl.semaphore_signal(barrier, inc=1, device_id={"head": lax.rem(x + k, nx)}, device_id_type=MESH)
+
+    pl.semaphore_wait(barrier, jnp.where(place == 0, nx - 1, 1))
 
     @pl.when(place < nz - 1)
     def _():
         pl.semaphore_signal(barrier, inc=1, device_id={"seq": up}, device_id_type=MESH)
+
+    for i in (1, 2):
+
+        @pl.when(place >= i)
+        def _(i=i):
+            pl.semaphore_signal(go.at[i], inc=1, device_id={"seq": lax.rem(z + nz - i, nz)}, device_id_type=MESH)
 
     rows = tokens.shape[0]
     feats = tokens.shape[1]
@@ -176,19 +182,27 @@
 
     up_to[...] = q_buf[0]
 
-    @pl.when(place > 0)
-    def _():
-        pltpu.make_async_copy(below, below, r_up).wait()
-        up_to[...] = q_buf[0] + below[...]
+    @pl.when(place >= 2)
+    def _():
+        pltpu.make_async_copy(below.at[1], below.at[1], r_up.at[1]).wait()
+        up_to[...] = q_buf[0] + below[1]
 
     total_q[...] = up_to[...]
 
-    @pl.when(place < nz - 1)
-    def _():
-        pl.semaphore_wait(go, 1)
-        pltpu.make_async_remote_copy(
-            src_ref=up_to, dst_ref=below, send_sem=s_up, recv_sem=r_up, device_id={"seq": up}, device_id_type=MESH,
-        ).start()
+    for i in (1, 2):
+
+        @pl.when(place < nz - i)
+        def _(i=i):
+            pl.semaphore_wait(go.at[i], 1)
+            pltpu.make_async_remote_copy(
+                src_ref=up_to, dst_ref=below.at[i - 1], send_sem=s_up.at[i - 1], recv_sem=r_up.at[i - 1],
+                device_id={"seq": lax.rem(z + i, nz)}, device_id_type=MESH,
+            ).start()
+
+    @pl.when(place >= 1)
+    def _():
+        pltpu.make_async_copy(below.at[0], below.at[0], r_up.at[0]).wait()
+        total_q[...] += below[0]
 
     for k in range(1, nz):
 
@@ -196,6 +210,11 @@
         def _(k=k):
             pltpu.make_async_copy(q_buf.at[k], q_buf.at[k], r_q.at[k]).wait()
             total_q[...] += q_buf[k]
+
+    @pl.when(place == 0)
+    def _():
+        for k in far_first(nx):
+            pl.semaphore_signal(ready_x, inc=1, device_id={"head": lax.rem(x + k, nx)}, device_id_type=MESH)
 
     r_a = lax.rsqrt(total_q[:, qw:] / width + NORM_EPS)
 
@@ -235,6 +254,13 @@
     send_all("seq", nz, aux_buf, s_aux, r_aux)
     send_all("seq", nz, acc_buf, s_acc, r_acc)
 
+    @pl.when(place == 0)
+    def _():
+        pl.semaphore_wait(ready_x, nx - 1)
+        for k in far_first(nz):
+            pl.semaphore_signal(ready, inc=1, device_id={"seq": lax.rem(z + k, nz)}, device_id_type=MESH)
+
+
     need("w_out")
     wait_for(aux_buf, r_aux, nz - 1)
     aux = jnp.concatenate([aux_buf[k] for k in range(nz)], axis=0)
@@ -249,6 +275,11 @@
         attended = attended + share[:qrows, k : k + 1] * acc_buf[k].astype(F32)
     attended = jnp.concatenate([attended[g * rows : (g + 1) * rows] for g in range(groups)], axis=1).astype(BF16)
     part_buf[0] = dot(attended, w_out[...]).astype(BF16)
+
+    @pl.when(place > 0)
+    def _():
+        pl.semaphore_wait(ready, 1)
+
     send_all("head", nx, part_buf, s_part, r_part)
     need("mamba_gain", "w_in")
     wait_for(part_buf, r_part, nx - 1)
@@ -344,9 +375,11 @@
     def _():
         pltpu.make_async_copy(kv_buf.at[0], kv_buf.at[0], s_kv).wait()
 
-    @pl.when(place < nz - 1)
-    def _():
-        pltpu.make_async_copy(up_to, up_to, s_up).wait()
+    for i in (1, 2):
+
+        @pl.when(place < nz - i)
+        def _(i=i):
+            pltpu.make_async_copy(up_to, up_to, s_up.at[i - 1]).wait()
 
     wait_for(aux_buf, s_aux, nz - 1)
     wait_for(acc_buf, s_acc, nz - 1)
@@ -394,7 +427,7 @@
     dma = pltpu.SemaphoreType.DMA
     buffers = [
         ((nz, rows, w_query.shape[1] + 128), F32),
-        ((rows, w_query.shape[1] + 128), F32),
+        ((2, rows, w_query.shape[1] + 128), F32),
         ((rows, w_query.shape[1] + 128), F32),
         ((rows, w_query.shape[1] + 128), F32),
         ((nz, rows, 2 * hd), F32),
@@ -410,7 +443,8 @@
         ((nz, rows, feats), BF16),
         ((nx, rows, feats), F32),
     ]
-    sems = [dma((nz,)), dma((nz,)), dma, dma, pltpu.SemaphoreType.REGULAR] + [dma] * 8 + [dma, dma((3,))] + [dma] * 8
+    flag = pltpu.SemaphoreType.REGULAR
+    sems = [dma((nz,)), dma((nz,)), dma((2,)), dma((2,)), flag((3,)), flag, flag] + [dma] * 8 + [dma, dma((3,))] + [dma] * 8
     hidden, state = pl.pallas_call(
         functools.partial(kernel, nz, nx),
         out_shape=(

time: 108 us -> 107 us (level)
  no operation moved by 1% of the time
where the time goes in v3:
time: 107 us
  Pallas kernels  106 us (99%)
    pallas_call x1, Pallas kernels, local(): pl.pallas_call(functools.partial(kernel, nz, nx), out_shape=(pltpu.VMEM((...  106 us

profile of v3, /device:TPU:80, one launch (start us, length us, event | category | flops | bytes accessed | tf_op | source)
XLA Modules:
  0.0 106.9 jit_solution(10455673005877638710)
XLA Ops:
  0.6 105.6 %decode_step.1 = (bf16[8,256]{1,0:T(8,128)(2,1)S(1)}, f32[8,16,64]{2,1,0:T(8,128)S(1)}) custom-call(bf16[8,256]{1,0:T(8,128)(2,1)} %refs_0_.1, f32[1,256]{1,0:T(1,128)} %bitcast.20, bf16[256,512]{1,0:T(8,128)(2,1)} %refs_2_.1, bf16[256,128]{1,0:T(8,128)(2,1)} %refs_3_.1, bf16[256,128]{1,0:T(8,128)(2,1)} %refs_4_.1, bf16[512,256]{1,0:T(8,128)(2,1)} %refs_5_.1, ...), custom_call_target="tpu_custom_call" | custom-call | tf_op jit(solution)/shard_map/decode_step/pallas_call | solution.py:448
  106.3 0.7 put_out.1

commit v4 on v3

--- a/solution.py
+++ b/solution.py
@@ -96,6 +96,12 @@
         conv_state=(conv_state_h, conv_state), w_xproj=(w_xproj_h, w_xproj), w_dt=(w_dt_h, w_dt), dt_bias=(dt_bias_h, dt_bias),
         a_log=(a_log_h, a_log), skip_gain=(skip_gain_h, skip_gain), ssm=(ssm_h, ssm), w_mout=(w_mout_h, w_mout),
     )
+    quarter = w_query.shape[0] // 4
+    del pairs["w_query"]
+    for i in range(4):
+        part = pl.ds(i * quarter, quarter)
+        loads["w_query", i] = pltpu.make_async_copy(w_query_h.at[part], w_query.at[part], load_sem.at[len(pairs) + i])
+        loads["w_query", i].start()
     for i, (name, (source, target)) in enumerate(pairs.items()):
         loads[name] = pltpu.make_async_copy(source, target, load_sem.at[i])
         loads[name].start()
@@ -134,12 +140,22 @@
     rank = w_dt.shape[1]
     nstate = a_log.shape[0]
 
-    need("tokens", "attn_gain", "w_query")
+    need("tokens", "attn_gain", *[("w_query", i) for i in range(4)])
     token_f = tokens[...].astype(F32)
     lifted = (token_f * attn_gain[...]).astype(BF16)
     qw = w_query.shape[1]
-    q_buf[0, :, :qw] = dot(lifted, w_query[...])
-    q_buf[0, :, qw:] = jnp.broadcast_to(jnp.sum(token_f * token_f, axis=1, keepdims=True), (rows, 128))
+    part = dot(lifted, w_query[...])
+    q_buf[0, :, :qw] = part.astype(BF16)
+    left = jnp.sum(token_f * token_f, axis=1, keepdims=True)
+    lane = lax.broadcasted_iota(jnp.int32, (rows, 128), 1)
+    up_to[:, :qw] = part
+    up_to[:, qw:] = jnp.where(lane == 0, left, 0.0)
+    terms = jnp.zeros((rows, 128), F32)
+    for i in range(3):
+        term = left.astype(BF16).astype(F32)
+        terms = jnp.where(lane == i, term, terms)
+        left = left - term
+    q_buf[0, :, qw:] = terms.astype(BF16)
 
     for k in far_first(nz):
 
@@ -180,12 +196,10 @@
     row_of = lax.broadcasted_iota(jnp.int32, (qrows, hd), 0) % rows
     row_of_wide = lax.broadcasted_iota(jnp.int32, (qrows, span), 0) % rows
 
-    up_to[...] = q_buf[0]
-
     @pl.when(place >= 2)
     def _():
         pltpu.make_async_copy(below.at[1], below.at[1], r_up.at[1]).wait()
-        up_to[...] = q_buf[0] + below[1]
+        up_to[...] += below[1]
 
     total_q[...] = up_to[...]
 
@@ -209,14 +223,14 @@
         @pl.when(place + k < nz)
         def _(k=k):
             pltpu.make_async_copy(q_buf.at[k], q_buf.at[k], r_q.at[k]).wait()
-            total_q[...] += q_buf[k]
+            total_q[...] += q_buf[k].astype(F32)
 
     @pl.when(place == 0)
     def _():
         for k in far_first(nx):
             pl.semaphore_signal(ready_x, inc=1, device_id={"head": lax.rem(x + k, nx)}, device_id_type=MESH)
 
-    r_a = lax.rsqrt(total_q[:, qw:] / width + NORM_EPS)
+    r_a = lax.rsqrt(jnp.sum(total_q[:, qw:], axis=1, keepdims=True) / width + NORM_EPS)
 
     @pl.when(is_owner)
     def _():
@@ -426,7 +440,7 @@
     pad = -(-w_xproj.shape[1] // 128) * 128
     dma = pltpu.SemaphoreType.DMA
     buffers = [
-        ((nz, rows, w_query.shape[1] + 128), F32),
+        ((nz, rows, w_query.shape[1] + 128), BF16),
         ((2, rows, w_query.shape[1] + 128), F32),
         ((rows, w_query.shape[1] + 128), F32),
         ((rows, w_query.shape[1] + 128), F32),
@@ -454,7 +468,7 @@
         in_specs=[pl.BlockSpec(memory_space=pltpu.HBM)] * len(operands),
         out_specs=(pl.BlockSpec(memory_space=pltpu.VMEM), pl.BlockSpec(memory_space=pltpu.VMEM)),
         scratch_shapes=[pltpu.VMEM(o.shape, o.dtype) for o in operands]
-        + [dma((len(operands),))]
+        + [dma((len(operands) + 3,))]
         + [pltpu.VMEM(shape, kind) for shape, kind in buffers]
         + sems,
         compiler_params=pltpu.CompilerParams(

time: 107 us -> 101 us (0.944)
  Pallas kernels: 106 us -> 100 us
    pallas_call x1, Pallas kernels: 106 us -> 99.4 us  [local(): pl.pallas_call(functools.partial(kernel, nz, nx), out_shape=(pltpu.VMEM((...]
where the time goes in v4:
time: 101 us
  Pallas kernels  100 us (99%)
    pallas_call x1, Pallas kernels, local(): pl.pallas_call(functools.partial(kernel, nz, nx), out_shape=(pltpu.VMEM((...  99.4 us

profile of v4, /device:TPU:80, one launch (start us, length us, event | category | flops | bytes accessed | tf_op | source)
XLA Modules:
  0.0 100.7 jit_solution(9054213025848820595)
XLA Ops:
  0.6 99.4 %decode_step.1 = (bf16[8,256]{1,0:T(8,128)(2,1)S(1)}, f32[8,16,64]{2,1,0:T(8,128)S(1)}) custom-call(bf16[8,256]{1,0:T(8,128)(2,1)} %refs_0_.1, f32[1,256]{1,0:T(1,128)} %bitcast.20, bf16[256,512]{1,0:T(8,128)(2,1)} %refs_2_.1, bf16[256,128]{1,0:T(8,128)(2,1)} %refs_3_.1, bf16[256,128]{1,0:T(8,128)(2,1)} %refs_4_.1, bf16[512,256]{1,0:T(8,128)(2,1)} %refs_5_.1, ...), custom_call_target="tpu_custom_call" | custom-call | tf_op jit(solution)/shard_map/decode_step/pallas_call | solution.py:462
  100.0 0.7 put_out.1

commit v5 on v4

--- a/solution.py
+++ b/solution.py
@@ -46,6 +46,21 @@
 def row_to_column(row, rows):
     spread = jnp.where(diagonal((rows, row.shape[1])), jnp.broadcast_to(row, (rows, row.shape[1])), 0.0)
     return jnp.sum(spread, axis=1, keepdims=True)
+
+
+def in_terms(row, count):
+    lane = lax.broadcasted_iota(jnp.int32, row.shape, 1)
+    left = jnp.where(lane < count, row, 0.0)
+    terms = jnp.zeros_like(row)
+    for i in range(3):
+        term = left.astype(BF16).astype(F32)
+        terms = terms + (pltpu.roll(term, i * count, 1) if i else term)
+        left = left - term
+    return terms
+
+
+def of_terms(terms, count):
+    return terms + pltpu.roll(terms, 128 - count, 1) + pltpu.roll(terms, 128 - 2 * count, 1)
 
 
 def send_all(axis, n, buffer, send_sem, recv_sem):
@@ -76,14 +91,15 @@
         mamba_gain, w_in, conv_weight, conv_bias, conv_state, w_xproj, w_dt, dt_bias, a_log,
         skip_gain, ssm, w_mout, freq,
         load_sem,
-        q_buf, below, up_to, total_q, kv_buf, knew, vnew, acc_buf, aux_buf, part_buf, mid_buf, px_buf, pz_buf,
+        q_buf, below, up_to, total_q, kv_buf, knew, vnew, acc_buf, part_buf, mid_buf, px_buf, pz_buf,
         out_src, share_buf, fin_buf,
-        s_q, r_q, s_up, r_up, go, ready_x, ready, s_kv, r_kv, s_acc, r_acc, s_aux, r_aux, s_part, r_part, s_mid, r_mid,
+        s_q, r_q, s_up, r_up, go, ready_x, ready, s_kv, r_kv, s_acc, r_acc, s_part, r_part, s_mid, r_mid,
         s_px, r_px, s_pz, r_pz, s_sh, r_sh, s_fin, r_fin,
     ) = refs
     z = lax.axis_index("seq")
     x = lax.axis_index("head")
-    place = lax.rem(z + nz - 1, nz)
+    first = jnp.where(x == 0, 1, 0)
+    place = lax.rem(z + nz - first, nz)
     up = lax.rem(z + 1, nz)
     is_owner = place == 0
 
@@ -112,10 +128,15 @@
 
     barrier = pltpu.get_barrier_semaphore()
 
+    def hub(k):
+        peer = lax.rem(x + k, nx)
+        return {"head": peer, "seq": jnp.where(peer == 0, 1, 0)}
+
+
     @pl.when(place == 0)
     def _():
         for k in far_first(nx):
-            pl.semaphore_signal(barrier, inc=1, device_id={"head": lax.rem(x + k, nx)}, device_id_type=MESH)
+            pl.semaphore_signal(barrier, inc=1, device_id=hub(k), device_id_type=MESH)
 
     pl.semaphore_wait(barrier, jnp.where(place == 0, nx - 1, 1))
 
@@ -174,7 +195,7 @@
     def _():
         pltpu.make_async_remote_copy(
             src_ref=kv_buf.at[0], dst_ref=kv_buf.at[place], send_sem=s_kv, recv_sem=r_kv,
-            device_id={"seq": 1}, device_id_type=MESH,
+            device_id={"seq": first}, device_id_type=MESH,
         ).start()
 
     knew[...] = jnp.zeros_like(knew)
@@ -228,7 +249,7 @@
     @pl.when(place == 0)
     def _():
         for k in far_first(nx):
-            pl.semaphore_signal(ready_x, inc=1, device_id={"head": lax.rem(x + k, nx)}, device_id_type=MESH)
+            pl.semaphore_signal(ready_x, inc=1, device_id=hub(k), device_id_type=MESH)
 
     r_a = lax.rsqrt(jnp.sum(total_q[:, qw:], axis=1, keepdims=True) / width + NORM_EPS)
 
@@ -263,9 +284,8 @@
     for b in range(rows):
         acc = jnp.where(row_of == b, dot(weights, values[b]), acc)
     acc = acc + new_weight * jnp.concatenate([vnew[...]] * groups, axis=0)
-    acc_buf[0] = acc.astype(BF16)
-    aux_buf[0] = column_to_row(top) + pltpu.roll(column_to_row(total), 64, 1)
-    send_all("seq", nz, aux_buf, s_aux, r_aux)
+    acc_buf[0, :qrows] = acc.astype(BF16)
+    acc_buf[0, qrows:] = jnp.concatenate([in_terms(column_to_row(top), qrows), in_terms(column_to_row(total), qrows)]).astype(BF16)
     send_all("seq", nz, acc_buf, s_acc, r_acc)
 
     @pl.when(place == 0)
@@ -276,17 +296,18 @@
 
 
     need("w_out")
-    wait_for(aux_buf, r_aux, nz - 1)
-    aux = jnp.concatenate([aux_buf[k] for k in range(nz)], axis=0)
-    factor = jnp.exp(aux - jnp.max(aux, axis=0, keepdims=True))
-    whole = jnp.sum(factor * pltpu.roll(aux, 64, 1), axis=0, keepdims=True)
+    wait_for(acc_buf, r_acc, nz - 1)
+    aux = [acc_buf[k, qrows:].astype(F32) for k in range(nz)]
+    tops = of_terms(jnp.concatenate([a[:1] for a in aux], axis=0), qrows)
+    sums = of_terms(jnp.concatenate([a[1:] for a in aux], axis=0), qrows)
+    factor = jnp.exp(tops - jnp.max(tops, axis=0, keepdims=True))
+    whole = jnp.sum(factor * sums, axis=0, keepdims=True)
     lane = lax.broadcasted_iota(jnp.int32, (nz, 128), 1)
     share = jnp.where(lane < qrows, factor / whole, 0.0)
     share = jnp.concatenate([share, jnp.zeros((128 - nz, 128), F32)], axis=0).T
-    wait_for(acc_buf, r_acc, nz - 1)
-    attended = share[:qrows, 0:1] * acc_buf[0].astype(F32)
+    attended = share[:qrows, 0:1] * acc_buf[0, :qrows].astype(F32)
     for k in range(1, nz):
-        attended = attended + share[:qrows, k : k + 1] * acc_buf[k].astype(F32)
+        attended = attended + share[:qrows, k : k + 1] * acc_buf[k, :qrows].astype(F32)
     attended = jnp.concatenate([attended[g * rows : (g + 1) * rows] for g in range(groups)], axis=1).astype(BF16)
     part_buf[0] = dot(attended, w_out[...]).astype(BF16)
 
@@ -395,7 +416,6 @@
         def _(i=i):
             pltpu.make_async_copy(up_to, up_to, s_up.at[i - 1]).wait()
 
-    wait_for(aux_buf, s_aux, nz - 1)
     wait_for(acc_buf, s_acc, nz - 1)
     wait_for(part_buf, s_part, nx - 1)
     wait_for(mid_buf, s_mid, nz - 1)
@@ -447,8 +467,7 @@
         ((nz, rows, 2 * hd), F32),
         ((rows, hd), F32),
         ((rows, hd), F32),
-        ((nz, qrows, hd), BF16),
-        ((nz, 1, 128), F32),
+        ((nz, qrows + 2, hd), BF16),
         ((nx, rows, feats), BF16),
         ((nz, rows, feats), BF16),
         ((nx, rows, pad), BF16),
@@ -458,7 +477,7 @@
         ((nx, rows, feats), F32),
     ]
     flag = pltpu.SemaphoreType.REGULAR
-    sems = [dma((nz,)), dma((nz,)), dma((2,)), dma((2,)), flag((3,)), flag, flag] + [dma] * 8 + [dma, dma((3,))] + [dma] * 8
+    sems = [dma((nz,)), dma((nz,)), dma((2,)), dma((2,)), flag((3,)), flag, flag] + [dma] * 6 + [dma, dma((3,))] + [dma] * 8
     hidden, state = pl.pallas_call(
         functools.partial(kernel, nz, nx),
         out_shape=(

time: 101 us -> 101 us (level)
  no operation moved by 1% of the time
where the time goes in v5:
time: 101 us; the launch traced here: 100 us
  Pallas kernels  99.8 us (99%)
    pallas_call x1, Pallas kernels, local(): pl.pallas_call(functools.partial(kernel, nz, nx), out_shape=(pltpu.VMEM((...  99.1 us

profile of v5, /device:TPU:80, one launch (start us, length us, event | category | flops | bytes accessed | tf_op | source)
XLA Modules:
  0.0 100.4 jit_solution(5975300716882061152)
XLA Ops:
  0.6 99.1 %decode_step.1 = (bf16[8,256]{1,0:T(8,128)(2,1)S(1)}, f32[8,16,64]{2,1,0:T(8,128)S(1)}) custom-call(bf16[8,256]{1,0:T(8,128)(2,1)} %refs_0_.1, f32[1,256]{1,0:T(1,128)} %bitcast.20, bf16[256,512]{1,0:T(8,128)(2,1)} %refs_2_.1, bf16[256,128]{1,0:T(8,128)(2,1)} %refs_3_.1, bf16[256,128]{1,0:T(8,128)(2,1)} %refs_4_.1, bf16[512,256]{1,0:T(8,128)(2,1)} %refs_5_.1, ...), custom_call_target="tpu_custom_call" | custom-call | tf_op jit(solution)/shard_map/decode_step/pallas_call | solution.py:481
  99.8 0.7 put_out.1

commit v6 on v5

--- a/solution.py
+++ b/solution.py
@@ -91,7 +91,7 @@
         mamba_gain, w_in, conv_weight, conv_bias, conv_state, w_xproj, w_dt, dt_bias, a_log,
         skip_gain, ssm, w_mout, freq,
         load_sem,
-        q_buf, below, up_to, total_q, kv_buf, knew, vnew, acc_buf, part_buf, mid_buf, px_buf, pz_buf,
+        turned, q_buf, below, up_to, total_q, kv_buf, knew, vnew, acc_buf, part_buf, mid_buf, px_buf, pz_buf,
         out_src, share_buf, fin_buf,
         s_q, r_q, s_up, r_up, go, ready_x, ready, s_kv, r_kv, s_acc, r_acc, s_part, r_part, s_mid, r_mid,
         s_px, r_px, s_pz, r_pz, s_sh, r_sh, s_fin, r_fin,
@@ -234,6 +234,10 @@
                 device_id={"seq": lax.rem(z + i, nz)}, device_id_type=MESH,
             ).start()
 
+    need("keys")
+    for b in range(rows):
+        turned[b * hd : (b + 1) * hd] = keys[b].T
+
     @pl.when(place >= 1)
     def _():
         pltpu.make_async_copy(below.at[0], below.at[0], r_up.at[0]).wait()
@@ -265,24 +269,20 @@
     q = [rotated(total_q[:, g * hd : (g + 1) * hd] * r_a) for g in range(groups)]
     q = jnp.concatenate(q, axis=0).astype(BF16)
 
-    need("keys")
-    scores = jnp.zeros((qrows, span), F32)
-    for b in range(rows):
-        scores = jnp.where(row_of_wide == b, dot_t(q, keys[b]), scores)
+    q = q.astype(F32)
     scale = hd ** (-0.5)
+    scores = dot(jnp.concatenate([jnp.where(row_of == b, q, 0.0).astype(BF16) for b in range(rows)], axis=1), turned[...])
     scores = scores * scale
     top = jnp.max(jnp.where(live, scores, FLOOR), axis=1, keepdims=True)
-    fresh = jnp.sum(q.astype(F32) * jnp.concatenate([knew[...]] * groups, axis=0), axis=1, keepdims=True) * scale
+    fresh = jnp.sum(q * jnp.concatenate([knew[...]] * groups, axis=0), axis=1, keepdims=True) * scale
     mine = jnp.broadcast_to(is_owner, fresh.shape)
     top = jnp.maximum(top, jnp.where(mine, fresh, FLOOR))
     weights = jnp.where(live, jnp.exp(scores - top), 0.0)
     new_weight = jnp.where(mine, jnp.exp(fresh - top), 0.0)
     total = jnp.sum(weights, axis=1, keepdims=True) + new_weight
-    weights = weights.astype(BF16)
+    weights = jnp.concatenate([jnp.where(row_of_wide == b, weights, 0.0).astype(BF16) for b in range(rows)], axis=1)
     need("values")
-    acc = jnp.zeros((qrows, hd), F32)
-    for b in range(rows):
-        acc = jnp.where(row_of == b, dot(weights, values[b]), acc)
+    acc = dot(weights, values[...].reshape(rows * span, hd))
     acc = acc + new_weight * jnp.concatenate([vnew[...]] * groups, axis=0)
     acc_buf[0, :qrows] = acc.astype(BF16)
     acc_buf[0, qrows:] = jnp.concatenate([in_terms(column_to_row(top), qrows), in_terms(column_to_row(total), qrows)]).astype(BF16)
@@ -304,7 +304,7 @@
     whole = jnp.sum(factor * sums, axis=0, keepdims=True)
     lane = lax.broadcasted_iota(jnp.int32, (nz, 128), 1)
     share = jnp.where(lane < qrows, factor / whole, 0.0)
-    share = jnp.concatenate([share, jnp.zeros((128 - nz, 128), F32)], axis=0).T
+    share = share.T
     attended = share[:qrows, 0:1] * acc_buf[0, :qrows].astype(F32)
     for k in range(1, nz):
         attended = attended + share[:qrows, k : k + 1] * acc_buf[k, :qrows].astype(F32)
@@ -370,7 +370,7 @@
 
     pre = dot_t(proj[:, :rank].astype(BF16), w_dt[...]) + dt_bias[...]
     step = jnp.maximum(pre, 0.0) + jnp.log(1.0 + jnp.exp(-jnp.abs(pre)))
-    maps = jnp.concatenate([proj[:, rank : rank + 128], jnp.zeros((128 - rows, 128), F32)], axis=0).T
+    maps = proj[:, rank : rank + 128].T
     drive = step * u
     reads = []
     for b in range(rows):
@@ -460,6 +460,7 @@
     pad = -(-w_xproj.shape[1] // 128) * 128
     dma = pltpu.SemaphoreType.DMA
     buffers = [
+        ((rows * hd, span), BF16),
         ((nz, rows, w_query.shape[1] + 128), BF16),
         ((2, rows, w_query.shape[1] + 128), F32),
         ((rows, w_query.shape[1] + 128), F32),

time: 101 us -> 100 us (0.990)
  no operation moved by 1% of the time
where the time goes in v6:
time: 100 us
  Pallas kernels  99.5 us (100%)
    pallas_call x1, Pallas kernels, local(): pl.pallas_call(functools.partial(kernel, nz, nx), out_shape=(pltpu.VMEM((...  98.9 us

profile of v6, /device:TPU:80, one launch (start us, length us, event | category | flops | bytes accessed | tf_op | source)
XLA Modules:
  0.0 100.2 jit_solution(2879042828888393578)
XLA Ops:
  0.6 98.9 %decode_step.1 = (bf16[8,256]{1,0:T(8,128)(2,1)S(1)}, f32[8,16,64]{2,1,0:T(8,128)S(1)}) custom-call(bf16[8,256]{1,0:T(8,128)(2,1)} %refs_0_.1, f32[1,256]{1,0:T(1,128)} %bitcast.20, bf16[256,512]{1,0:T(8,128)(2,1)} %refs_2_.1, bf16[256,128]{1,0:T(8,128)(2,1)} %refs_3_.1, bf16[256,128]{1,0:T(8,128)(2,1)} %refs_4_.1, bf16[512,256]{1,0:T(8,128)(2,1)} %refs_5_.1, ...), custom_call_target="tpu_custom_call" | custom-call | tf_op jit(solution)/shard_map/decode_step/pallas_call | solution.py:482
  99.5 0.7 put_out.1
